TPU v7x, 32 devices: a whole 2x2x4 slice. The times are simulated.
32 devices in a mesh: gx: 8 (over z, y), gy: 4 (over x, core).
Axes of the slice: x: 2, y: 2, z: 4, core: 2. Of those that a mesh axis runs over, the one named last changes fastest.
Arguments:
- right_side: float32 [64, 128, 128], P('gy', 'gx'), may hold values from -6 to 9
- diagonal: float32 [64, 128, 128], P('gy', 'gx'), may hold values from 0.02 to 0.5
- horizontal: float32 [64, 128, 128], P('gy', 'gx'), may hold values from 0.1 to 1
- vertical: float32 [128], replicated, may hold values from 0.2 to 2
- precond: float32 [2, 128, 128], replicated, may hold values from -4 to 4
- edge_rows: int32 [2, 64], replicated, may hold values from 0 to 63, as said below
Outputs:
- solution_field: float32 [64, 128, 128], P('gy', 'gx')
- residual: float32 [64, 128, 128], P('gy', 'gx')
- residual_sq: float32 [3], replicated
Inputs may be any that keep to these rules, and one draw needn't show every extreme that they name: Each row of edge_rows lists every number 0 to 63 exactly once.
All inputs are finite; a program needn't handle non-finite values.
Results may differ from a plain program's by a relative error of at most 0.00014.
Values sent between devices are 32-bit elements; how exact they have to be, the bound alone decides.
A program may use at most 64 MiB of HBM per device.

v0:
```python
import jax
import jax.numpy as jnp
from jax import lax
from jax.sharding import PartitionSpec as P

ITERS = 3


def padded(x, sides, width, wrap):
    for axis, dim in sides:
        devices, length = (lax.axis_size(axis), x.shape[dim])
        up = [(i, (i + 1) % devices) for i in range(devices if wrap else devices - 1)]
        down = [(j, i) for i, j in up]
        last = lax.slice_in_dim(x, length - width, length, axis=dim)
        initial = lax.slice_in_dim(x, 0, width, axis=dim)
        before = lax.ppermute(last, axis, up)
        after = lax.ppermute(initial, axis, down)
        x = jnp.concatenate([before, x, after], axis=dim)
    return x


def local_product(left, right):
    return jnp.sum(left * right)


def on_device(right_side, diagonal, horizontal, vertical, precond, edge_rows):
    rows, cols, levels = right_side.shape
    n_gx = lax.axis_size("gx")
    n_gy = lax.axis_size("gy")
    col_index = lax.axis_index("gx")
    row_index = lax.axis_index("gy")
    total_cells = float(rows * cols * levels * n_gx * n_gy)
    half = n_gx // 2
    panel = (col_index >= half).astype(jnp.int32)
    matrix = lax.dynamic_index_in_dim(precond, panel, 0, keepdims=False)
    east_table = jnp.where(col_index == half - 1, edge_rows[0], edge_rows[1])
    west_table = jnp.where(col_index == half, edge_rows[0], edge_rows[1])
    first_row = row_index * rows
    east_local = lax.dynamic_slice_in_dim(east_table, first_row, rows)
    west_local = lax.dynamic_slice_in_dim(west_table, first_row, rows)
    east_border = (col_index == half - 1) | (col_index == n_gx - 1)
    west_border = (col_index == half) | (col_index == 0)
    solution_field = jnp.zeros_like(right_side)
    residual = right_side
    directions = []
    images = []
    norms = []
    for step in range(ITERS):
        pre = jnp.einsum("yxl,kl->yxk", residual, matrix, precision=lax.Precision.HIGHEST)
        wide = padded(pre, (("gx", 1),), 1, True)
        edges = jnp.stack([wide[:, 0], wide[:, -1]], 0)
        whole = lax.all_gather(edges, "gy", axis=1, tiled=True)
        west_fix = jnp.take(whole[0], west_local, axis=0)
        east_fix = jnp.take(whole[1], east_local, axis=0)
        west = jnp.where(west_border, west_fix, edges[0])
        east = jnp.where(east_border, east_fix, edges[1])
        tall = padded(pre, (("gy", 0),), 1, False)
        flat = jnp.pad(pre, ((0, 0), (0, 0), (1, 1)))
        east_side = jnp.concatenate([pre[:, 1:], east[:, None]], 1)
        west_side = jnp.concatenate([west[:, None], pre[:, :-1]], 1)
        beside = east_side + west_side + tall[2:] + tall[:-2]
        column = flat[:, :, 2:] + flat[:, :, :-2]
        image = diagonal * pre + horizontal * (4.0 * pre - beside) + vertical * (2.0 * pre - column)
        count = len(images)
        terms = [local_product(image, older) for older in images]
        terms = terms + [local_product(residual, older) for older in images]
        terms = terms + [local_product(image, image), local_product(residual, image)]
        if step > 0:
            terms.append(local_product(residual, residual))
        totals = lax.psum(jnp.stack(terms), ("gx", "gy")) / total_cells
        coeffs = totals[:count]
        against = totals[count : 2 * count]
        square = totals[2 * count] - jnp.sum(coeffs * coeffs)
        along = totals[2 * count + 1] - jnp.sum(coeffs * against)
        if step > 0:
            norms.append(totals[2 * count + 2])
        for number in range(count):
            pre = pre - coeffs[number] * directions[number]
            image = image - coeffs[number] * images[number]
        scale = 1.0 / jnp.sqrt(square)
        alpha = along * scale
        direction = pre * scale
        image = image * scale
        solution_field = solution_field + alpha * direction
        residual = residual - alpha * image
        directions.append(direction)
        images.append(image)
    norms.append(lax.psum(local_product(residual, residual), ("gx", "gy")) / total_cells)
    return (solution_field, residual, jnp.stack(norms))


def solution(mesh):
    in_specs = (P("gy", "gx", None), P("gy", "gx", None), P("gy", "gx", None), P(), P(), P())
    out_specs = (P("gy", "gx", None), P("gy", "gx", None), P())
    return jax.shard_map(
        on_device, mesh=mesh, in_specs=in_specs, out_specs=out_specs, check_vma=False
    )
```

profile of v0, /device:TPU:0, one launch (start us, length us, event | category | flops | bytes accessed | tf_op | source)
XLA Modules:
  0.0 243.0 jit_solution(2497374235617542815)
XLA Ops:
  0.6 0.0 copy-start
  0.7 0.9 copy-done
  1.5 1.2 convolution_bitcast_fusion
  2.7 1.3 collective-permute-start.2
  4.0 3.0 %collective-permute-start.3 = (f32[1,16,128]{2,1,0:T(8,128)S(1)}, f32[1,16,128]{2,1,0:T(8,128)S(1)}, u32[]{:S(2)}, u32[]{:S(2)}) collective-permute-start(f32[1,16,128]{2,1,0:T(8,128)S(1)} %get-tuple-element.48), channel_id=1, source_target_pairs={{0,1},{1,2},{2,3},{4,5},{5,6},{6,7},{8,9},{9,10},{10,11},{12,13},{... | collective-permute-start | bytes 24584 | tf_op jit(solution)/shard_map/ppermute | solution.py:16
  7.1 3.0 %collective-permute-start = (f32[16,1,128]{2,0,1:T(8,128)S(1)}, f32[16,1,128]{2,0,1:T(8,128)S(1)}, u32[]{:S(2)}, u32[]{:S(2)}) collective-permute-start(f32[16,1,128]{2,0,1:T(8,128)S(1)} %bitcast.112), channel_id=1, source_target_pairs={{0,4},{4,8},{8,12},{12,16},{16,20},{20,24},{24,28},{28,0},{1,5},{5... | collective-permute-start | bytes 24584 | tf_op jit(solution)/shard_map/ppermute | solution.py:16
  10.1 3.1 %collective-permute-start.1 = (f32[16,1,128]{2,0,1:T(8,128)S(1)}, f32[16,1,128]{2,0,1:T(8,128)S(1)}, u32[]{:S(2)}, u32[]{:S(2)}) collective-permute-start(f32[16,1,128]{2,0,1:T(8,128)S(1)} %bitcast.111), channel_id=1, source_target_pairs={{4,0},{8,4},{12,8},{16,12},{20,16},{24,20},{28,24},{0,28},{5,1},{9... | collective-permute-start | bytes 24584 | tf_op jit(solution)/shard_map/ppermute | solution.py:17
  13.3 0.0 copy-start.5
  13.3 0.7 copy-done.5
  14.0 0.1 compare_and_fusion.1
  14.0 0.1 compare_and_fusion
  14.2 0.7 collective-permute-done
  14.8 0.0 collective-permute-done.1
  14.8 5.4 %all_gather.9 = f32[2,64,128]{2,1,0:T(8,128)S(1)} all-gather(f32[2,16,128]{2,1,0:T(8,128)S(1)} %pad_maximum_fusion.6), channel_id=1, replica_groups=mesh['gx'=8,'gy'=4] {'gy'}, dimensions={1}, use_global_device_ids=true | all-gather | bytes 81920 | tf_op jit(solution)/shard_map/all_gather | solution.py:52
  20.2 0.6 gather_fusion
  20.8 0.6 gather_fusion.1
  21.3 0.1 bitcast_select_fusion.5
  21.4 0.1 bitcast_select_fusion.4
  21.5 0.0 collective-permute-done.2
  21.5 0.0 collective-permute-done.3
  21.5 0.0 copy-start.4
  21.5 0.6 copy-done.4
  22.2 0.7 multiply_reduce_fusion.14
  22.9 1.4 pad_maximum_fusion.9
  24.3 40.2 %psum.28 = f32[2]{0:T(128)S(1)} all-reduce(f32[2]{0:T(128)S(1)} %pad_maximum_fusion.9), channel_id=1, replica_groups=mesh['gx'=8,'gy'=4] {'gx','gy'}, use_global_device_ids=true, to_apply=%region_2.4 | all-reduce | flops 2 | bytes 16 | tf_op jit(solution)/shard_map/psum | solution.py:70
  64.5 0.6 fusion.54
  66.5 0.3 fusion.29
  66.8 2.3 collective-permute-start.4
  69.1 2.5 %collective-permute-start.5 = (f32[16,1,128]{2,0,1:T(8,128)S(1)}, f32[16,1,128]{2,0,1:T(8,128)S(1)}, u32[]{:S(2)}, u32[]{:S(2)}) collective-permute-start(f32[16,1,128]{2,0,1:T(8,128)S(1)} %bitcast.113), channel_id=1, source_target_pairs={{4,0},{8,4},{12,8},{16,12},{20,16},{24,20},{28,24},{0,28},{5,1},{9... | collective-permute-start | bytes 24584 | tf_op jit(solution)/shard_map/ppermute | solution.py:17
  71.6 1.3 collective-permute-start.6
  72.9 3.0 %collective-permute-start.7 = (f32[1,16,128]{2,1,0:T(8,128)S(1)}, f32[1,16,128]{2,1,0:T(8,128)S(1)}, u32[]{:S(2)}, u32[]{:S(2)}) collective-permute-start(f32[1,16,128]{2,1,0:T(8,128)S(1)} %get-tuple-element.42), channel_id=1, source_target_pairs={{0,1},{1,2},{2,3},{4,5},{5,6},{6,7},{8,9},{9,10},{10,11},{12,13},{... | collective-permute-start | bytes 24584 | tf_op jit(solution)/shard_map/ppermute | solution.py:16
  75.9 0.0 collective-permute-done.4
  75.9 0.0 collective-permute-done.5
  75.9 5.8 %all_gather.10 = f32[2,64,128]{2,1,0:T(8,128)S(1)} all-gather(f32[2,16,128]{2,1,0:T(8,128)S(1)} %pad_maximum_fusion.7), channel_id=1, replica_groups=mesh['gx'=8,'gy'=4] {'gy'}, dimensions={1}, use_global_device_ids=true | all-gather | bytes 81920 | tf_op jit(solution)/shard_map/all_gather | solution.py:52
  81.8 0.6 gather_fusion.2
  82.3 0.6 gather_fusion.3
  82.9 0.1 bitcast_select_fusion.3
  83.0 0.1 bitcast_select_fusion.2
  83.0 0.0 collective-permute-done.6
  83.0 0.0 collective-permute-done.7
  83.1 0.8 multiply_reduce_fusion.8
  83.8 3.2 %stack.76 = f32[5]{0:T(128)S(1)} concatenate(f32[1]{0:T(128)} %bitcast.28, f32[1]{0:T(128)} %bitcast.29, f32[1]{0:T(128)} %bitcast.30, f32[1]{0:T(128)} %bitcast.31, f32[1]{0:T(128)} %bitcast.32), dimensions={0} | concatenate | bytes 40 | tf_op jit(solution)/shard_map/stack | solution.py:70
  87.1 37.9 %psum.29 = f32[5]{0:T(128)S(1)} all-reduce(f32[5]{0:T(128)S(1)} %stack.76), channel_id=1, replica_groups=mesh['gx'=8,'gy'=4] {'gx','gy'}, use_global_device_ids=true, to_apply=%region_8.10 | all-reduce | flops 5 | bytes 40 | tf_op jit(solution)/shard_map/psum | solution.py:70
  124.9 0.6 fusion.52
  129.4 0.7 multiply_subtract_fusion.1
  130.1 0.3 fusion.27
  130.4 2.3 collective-permute-start.8
  132.7 2.5 %collective-permute-start.9 = (f32[16,1,128]{2,0,1:T(8,128)S(1)}, f32[16,1,128]{2,0,1:T(8,128)S(1)}, u32[]{:S(2)}, u32[]{:S(2)}) collective-permute-start(f32[16,1,128]{2,0,1:T(8,128)S(1)} %bitcast.114), channel_id=1, source_target_pairs={{4,0},{8,4},{12,8},{16,12},{20,16},{24,20},{28,24},{0,28},{5,1},{9... | collective-permute-start | bytes 24584 | tf_op jit(solution)/shard_map/ppermute | solution.py:17
  135.2 1.3 collective-permute-start.10
  136.5 3.0 %collective-permute-start.11 = (f32[1,16,128]{2,1,0:T(8,128)S(1)}, f32[1,16,128]{2,1,0:T(8,128)S(1)}, u32[]{:S(2)}, u32[]{:S(2)}) collective-permute-start(f32[1,16,128]{2,1,0:T(8,128)S(1)} %get-tuple-element.36), channel_id=1, source_target_pairs={{0,1},{1,2},{2,3},{4,5},{5,6},{6,7},{8,9},{9,10},{10,11},{12,13},{... | collective-permute-start | bytes 24584 | tf_op jit(solution)/shard_map/ppermute | solution.py:16
  139.6 5.8 %all_gather.11 = f32[2,64,128]{2,1,0:T(8,128)S(1)} all-gather(f32[2,16,128]{2,1,0:T(8,128)S(1)} %pad_maximum_fusion.8), channel_id=1, replica_groups=mesh['gx'=8,'gy'=4] {'gy'}, dimensions={1}, use_global_device_ids=true | all-gather | bytes 81920 | tf_op jit(solution)/shard_map/all_gather | solution.py:52
  145.4 0.6 gather_fusion.4
  145.9 0.6 gather_fusion.5
  146.5 0.1 bitcast_select_fusion.1
  146.6 0.1 bitcast_select_fusion
  146.7 0.9 multiply_reduce_fusion.1
  147.5 4.5 %stack.85 = f32[7]{0:T(128)S(1)} concatenate(f32[1]{0:T(128)} %bitcast.46, f32[1]{0:T(128)} %bitcast.47, f32[1]{0:T(128)} %bitcast.48, f32[1]{0:T(128)} %bitcast.49, f32[1]{0:T(128)} %bitcast.50, f32[1]{0:T(128)} %bitcast.51, f32[1]{0:T(128)} %bitcast.52), dimensions={0} | concatenate | bytes 56 | tf_op jit(solution)/shard_map/stack | solution.py:70
  152.0 38.1 %psum.30 = f32[7]{0:T(128)S(1)} all-reduce(f32[7]{0:T(128)S(1)} %stack.85), channel_id=1, replica_groups=mesh['gx'=8,'gy'=4] {'gx','gy'}, use_global_device_ids=true, to_apply=%region_16.18 | all-reduce | flops 7 | bytes 56 | tf_op jit(solution)/shard_map/psum | solution.py:70
  190.1 0.8 multiply_reduce_fusion.16
  190.9 0.7 fusion.53
  194.1 2.6 %multiply_add_fusion = f32[16,16,128]{2,1,0:T(8,128)} fusion(f32[16,16,128]{2,1,0:T(8,128)S(1)} %fusion.27, f32[16,16,128]{2,1,0:T(8,128)S(1)} %fusion.29, f32[16,16,128]{2,1,0:T(8,128)S(1)} %convolution_bitcast_fusion, f32[]{:T(128)S(6)} %sqrt.17, f32[]{:T(128)} %bitcast.56, f32[]{:T(128)} %bitcast.55, f32[]{:T(128)S(6)} %mul.267, f32[]{:T(128)} %bitcast.34, ...), kind=kLoop, calls=%fused_computation.51 | loop fusion | flops 458752 | bytes 524324 | tf_op jit(solution)/shard_map/add | solution.py:84
  196.7 2.5 %multiply_reduce_fusion = (f32[]{:T(128)}, f32[16,16,128]{2,1,0:T(8,128)}) fusion(f32[16,16,128]{2,1,0:T(8,128)S(1)} %get-tuple-element.23, f32[]{:T(128)S(6)} %sqrt.17, f32[16,16,128]{2,1,0:T(8,128)S(1)} %get-tuple-element.24, f32[]{:T(128)} %bitcast.56, f32[16,16,128]{2,1,0:T(8,128)S(1)} %get-tuple-element.22, f32[16,16,128]{2,1,0:T(8,128)S(1)} %get-tuple-element.26, ...), kind=kLoop, calls=%fused_computation.49 | loop fusion | flops 327679 | bytes 655384 | tf_op jit(solution)/shard_map/reduce_sum | solution.py:23
  199.2 41.3 %psum.31 = f32[]{:T(128)} all-reduce(f32[]{:T(128)} %get-tuple-element.20), channel_id=1, replica_groups=mesh['gx'=8,'gy'=4] {'gx','gy'}, use_global_device_ids=true, to_apply=%region_20.22 | all-reduce | flops 1 | bytes 8 | tf_op jit(solution)/shard_map/psum | solution.py:88
  241.2 1.8 pad_maximum_fusion.10
  (32 shorter events, 0.2 us)
Async XLA Ops:
  0.6 0.9 copy-start
  2.7 18.8 %collective-permute-start.2 = (f32[1,16,128]{2,1,0:T(8,128)S(1)}, f32[1,16,128]{2,1,0:T(8,128)S(1)}, u32[]{:S(2)}, u32[]{:S(2)}) collective-permute-start(f32[1,16,128]{2,1,0:T(8,128)S(1)} %get-tuple-element.47), channel_id=1, source_target_pairs={{1,0},{2,1},{3,2},{5,4},{6,5},{7,6},{9,8},{10,9},{11,10},{13,12},{... | collective-permute-start | bytes 24584 | tf_op jit(solution)/shard_map/ppermute | solution.py:17
  4.0 17.5 %collective-permute-start.3 = (f32[1,16,128]{2,1,0:T(8,128)S(1)}, f32[1,16,128]{2,1,0:T(8,128)S(1)}, u32[]{:S(2)}, u32[]{:S(2)}) collective-permute-start(f32[1,16,128]{2,1,0:T(8,128)S(1)} %get-tuple-element.48), channel_id=1, source_target_pairs={{0,1},{1,2},{2,3},{4,5},{5,6},{6,7},{8,9},{9,10},{10,11},{12,13},{... | collective-permute-start | bytes 24584 | tf_op jit(solution)/shard_map/ppermute | solution.py:16
  7.1 7.7 %collective-permute-start = (f32[16,1,128]{2,0,1:T(8,128)S(1)}, f32[16,1,128]{2,0,1:T(8,128)S(1)}, u32[]{:S(2)}, u32[]{:S(2)}) collective-permute-start(f32[16,1,128]{2,0,1:T(8,128)S(1)} %bitcast.112), channel_id=1, source_target_pairs={{0,4},{4,8},{8,12},{12,16},{16,20},{20,24},{24,28},{28,0},{1,5},{5... | collective-permute-start | bytes 24584 | tf_op jit(solution)/shard_map/ppermute | solution.py:16
  10.1 4.7 %collective-permute-start.1 = (f32[16,1,128]{2,0,1:T(8,128)S(1)}, f32[16,1,128]{2,0,1:T(8,128)S(1)}, u32[]{:S(2)}, u32[]{:S(2)}) collective-permute-start(f32[16,1,128]{2,0,1:T(8,128)S(1)} %bitcast.111), channel_id=1, source_target_pairs={{4,0},{8,4},{12,8},{16,12},{20,16},{24,20},{28,24},{0,28},{5,1},{9... | collective-permute-start | bytes 24584 | tf_op jit(solution)/shard_map/ppermute | solution.py:17
  13.3 0.7 copy-start.5
  14.8 6.7 %copy-start.3 = (f32[16,16,128]{2,1,0:T(8,128)S(1)}, f32[16,16,128]{2,1,0:T(8,128)}, u32[]{:S(2)}) copy-start(f32[16,16,128]{2,1,0:T(8,128)} %param.9) | copy-start | bytes 393220
  20.2 1.3 copy-start.2
  20.2 1.3 copy-start.1
  21.5 0.7 copy-start.4
  66.8 9.1 %collective-permute-start.4 = (f32[16,1,128]{2,0,1:T(8,128)S(1)}, f32[16,1,128]{2,0,1:T(8,128)S(1)}, u32[]{:S(2)}, u32[]{:S(2)}) collective-permute-start(f32[16,1,128]{2,0,1:T(8,128)S(1)} %bitcast.115), channel_id=1, source_target_pairs={{0,4},{4,8},{8,12},{12,16},{16,20},{20,24},{24,28},{28,0},{1,5},{5... | collective-permute-start | bytes 24584 | tf_op jit(solution)/shard_map/ppermute | solution.py:16
  69.1 6.8 %collective-permute-start.5 = (f32[16,1,128]{2,0,1:T(8,128)S(1)}, f32[16,1,128]{2,0,1:T(8,128)S(1)}, u32[]{:S(2)}, u32[]{:S(2)}) collective-permute-start(f32[16,1,128]{2,0,1:T(8,128)S(1)} %bitcast.113), channel_id=1, source_target_pairs={{4,0},{8,4},{12,8},{16,12},{20,16},{24,20},{28,24},{0,28},{5,1},{9... | collective-permute-start | bytes 24584 | tf_op jit(solution)/shard_map/ppermute | solution.py:17
  71.6 11.5 %collective-permute-start.6 = (f32[1,16,128]{2,1,0:T(8,128)S(1)}, f32[1,16,128]{2,1,0:T(8,128)S(1)}, u32[]{:S(2)}, u32[]{:S(2)}) collective-permute-start(f32[1,16,128]{2,1,0:T(8,128)S(1)} %get-tuple-element.41), channel_id=1, source_target_pairs={{1,0},{2,1},{3,2},{5,4},{6,5},{7,6},{9,8},{10,9},{11,10},{13,12},{... | collective-permute-start | bytes 24584 | tf_op jit(solution)/shard_map/ppermute | solution.py:17
  72.9 10.2 %collective-permute-start.7 = (f32[1,16,128]{2,1,0:T(8,128)S(1)}, f32[1,16,128]{2,1,0:T(8,128)S(1)}, u32[]{:S(2)}, u32[]{:S(2)}) collective-permute-start(f32[1,16,128]{2,1,0:T(8,128)S(1)} %get-tuple-element.42), channel_id=1, source_target_pairs={{0,1},{1,2},{2,3},{4,5},{5,6},{6,7},{8,9},{9,10},{10,11},{12,13},{... | collective-permute-start | bytes 24584 | tf_op jit(solution)/shard_map/ppermute | solution.py:16
  130.4 9.1 %collective-permute-start.8 = (f32[16,1,128]{2,0,1:T(8,128)S(1)}, f32[16,1,128]{2,0,1:T(8,128)S(1)}, u32[]{:S(2)}, u32[]{:S(2)}) collective-permute-start(f32[16,1,128]{2,0,1:T(8,128)S(1)} %bitcast.116), channel_id=1, source_target_pairs={{0,4},{4,8},{8,12},{12,16},{16,20},{20,24},{24,28},{28,0},{1,5},{5... | collective-permute-start | bytes 24584 | tf_op jit(solution)/shard_map/ppermute | solution.py:16
  132.7 6.8 %collective-permute-start.9 = (f32[16,1,128]{2,0,1:T(8,128)S(1)}, f32[16,1,128]{2,0,1:T(8,128)S(1)}, u32[]{:S(2)}, u32[]{:S(2)}) collective-permute-start(f32[16,1,128]{2,0,1:T(8,128)S(1)} %bitcast.114), channel_id=1, source_target_pairs={{4,0},{8,4},{12,8},{16,12},{20,16},{24,20},{28,24},{0,28},{5,1},{9... | collective-permute-start | bytes 24584 | tf_op jit(solution)/shard_map/ppermute | solution.py:17
  135.2 11.5 %collective-permute-start.10 = (f32[1,16,128]{2,1,0:T(8,128)S(1)}, f32[1,16,128]{2,1,0:T(8,128)S(1)}, u32[]{:S(2)}, u32[]{:S(2)}) collective-permute-start(f32[1,16,128]{2,1,0:T(8,128)S(1)} %get-tuple-element.35), channel_id=1, source_target_pairs={{1,0},{2,1},{3,2},{5,4},{6,5},{7,6},{9,8},{10,9},{11,10},{13,12},{... | collective-permute-start | bytes 24584 | tf_op jit(solution)/shard_map/ppermute | solution.py:17
  136.5 10.2 %collective-permute-start.11 = (f32[1,16,128]{2,1,0:T(8,128)S(1)}, f32[1,16,128]{2,1,0:T(8,128)S(1)}, u32[]{:S(2)}, u32[]{:S(2)}) collective-permute-start(f32[1,16,128]{2,1,0:T(8,128)S(1)} %get-tuple-element.36), channel_id=1, source_target_pairs={{0,1},{1,2},{2,3},{4,5},{5,6},{6,7},{8,9},{9,10},{10,11},{12,13},{... | collective-permute-start | bytes 24584 | tf_op jit(solution)/shard_map/ppermute | solution.py:16
where the time goes:
time: 244 us; the launch traced here: 243 us
  blocking collectives  175 us (72%)
  starting transfers between devices  28.6 us (12%)
  local copies, waits for them, and re-layouts  15.2 us (6%)
  other arithmetic  12.7 us (5%)
  between operations  9.45 us (4%)
    psum x3, blocking collectives, on_device(): totals = lax.psum(jnp.stack(terms), ('gx', 'gy')) / total_cells  116 us
    psum x1, blocking collectives, on_device(): lax.psum(local_product(residual, residual), ('gx', 'gy')) / total_cells  41.3 us
    all_gather x3, blocking collectives, on_device(): whole = lax.all_gather(edges, 'gy', axis=1, tiled=True)  17 us
    ppermute x6, starting transfers between devices, padded(): before = lax.ppermute(last, axis, up)  16.8 us
    ppermute x6, starting transfers between devices, padded(): after = lax.ppermute(initial, axis, down)  11.9 us
    another operation x2, local copies, waits for them, and re-layouts, on_device(): totals = lax.psum(jnp.stack(terms), ('gx', 'gy')) / total_cells  7.69 us
    reduce_sum x4, other arithmetic, local_product(): return jnp.sum(left * right)  4.94 us
  transfers between devices with their start and end apart: 12, of which 1 were waited for; matrix products, arithmetic and copies ran while one was open for 2% of the time, Pallas kernels for 0%

commit v1 on v0

v1 whole, which is shorter than its diff:
```python
import functools

import jax
import jax.numpy as jnp
from jax import lax
from jax.experimental import pallas as pl
from jax.experimental.pallas import tpu as pltpu
from jax.sharding import PartitionSpec as P

ITERS = 3
MESH = pl.DeviceIdType.MESH
ANY = pl.BlockSpec(memory_space=pl.ANY)
VMEM = pl.BlockSpec(memory_space=pltpu.VMEM)
SMEM = pl.BlockSpec(memory_space=pltpu.SMEM)


def kernel(
    n_gx,
    n_gy,
    edge_rows,
    right_side,
    diagonal,
    horizontal,
    vertical,
    precond,
    out_x,
    out_r,
    out_norms,
    r0,
    diag,
    horiz,
    vert,
    matrix,
    fields,
    images,
    send_cols,
    from_east,
    from_west,
    from_north,
    from_south,
    east_col,
    west_col,
    sums,
    load_sem,
    col_send,
    east_recv,
    west_recv,
    row_send,
    north_recv,
    south_recv,
    sum_send,
    sum_recv,
):
    rows, cols, levels = r0.shape
    gx, gy = lax.axis_index("gx"), lax.axis_index("gy")
    n_all = n_gx * n_gy
    half = n_gx // 2
    me = gx * n_gy + gy
    total_cells = float(rows * cols * levels * n_all)

    def for_others(visit):
        for j in range(1, n_gy):
            visit(gx, lax.rem(gy + j, n_gy))

        def step(i, carry):
            for j in range(n_gy):
                visit(lax.rem(gx + i, n_gx), lax.rem(gy + j, n_gy))
            return carry

        if n_all <= 64:
            for i in range(1, n_gx):
                step(i, 0)
        else:
            lax.fori_loop(1, n_gx, step, 0)

    barrier = pltpu.get_barrier_semaphore()

    def greet(x, y):
        pl.semaphore_signal(barrier, inc=1, device_id=(x, y), device_id_type=MESH)

    for_others(greet)

    panel = lax.convert_element_type(gx >= half, jnp.int32)
    loads = [
        pltpu.make_async_copy(right_side, r0, load_sem.at[0]),
        pltpu.make_async_copy(precond.at[panel], matrix, load_sem.at[1]),
        pltpu.make_async_copy(diagonal, diag, load_sem.at[2]),
        pltpu.make_async_copy(horizontal, horiz, load_sem.at[3]),
        pltpu.make_async_copy(vertical, vert, load_sem.at[4]),
    ]
    for load in loads:
        load.start()

    east_x, west_x = lax.rem(gx + 1, n_gx), lax.rem(gx + n_gx - 1, n_gx)
    east_border = (gx == half - 1) | (gx == n_gx - 1)
    west_border = (gx == half) | (gx == 0)
    east_table = jnp.where(gx == half - 1, 0, 1)
    west_table = jnp.where(gx == half, 0, 1)
    first_row = gy * rows
    has_north, has_south = gy < n_gy - 1, gy > 0

    @pl.when(jnp.logical_not(has_north))
    def _():
        from_north[...] = jnp.zeros_like(from_north)

    @pl.when(jnp.logical_not(has_south))
    def _():
        from_south[...] = jnp.zeros_like(from_south)

    def flat(v):
        return v.reshape(rows * cols, levels)

    def precondition(v):
        return lax.dot_general(
            flat(v),
            matrix[...],
            (((1,), (1,)), ((), ())),
            precision=lax.Precision.HIGHEST,
            preferred_element_type=jnp.float32,
        ).reshape(rows, cols, levels)

    def col_copy(t, side, g):
        buffer, recv, x = (
            (from_west, west_recv, east_x) if side == 0 else (from_east, east_recv, west_x)
        )
        return pltpu.make_async_remote_copy(
            src_ref=send_cols.at[t, side],
            dst_ref=buffer[t].at[pl.ds(first_row, rows)],
            send_sem=col_send.at[t, side],
            recv_sem=recv.at[t],
            device_id=(x, g),
            device_id_type=MESH,
        )

    def row_copy(t, side):
        buffer, recv, y, row = (
            (from_south, south_recv, gy + 1, rows - 1)
            if side == 0
            else (from_north, north_recv, gy - 1, 0)
        )
        return pltpu.make_async_remote_copy(
            src_ref=fields.at[t, row],
            dst_ref=buffer.at[t],
            send_sem=row_send.at[t, side],
            recv_sem=recv.at[t],
            device_id=(gx, y),
            device_id_type=MESH,
        )

    def send(t):
        for side, border in ((0, east_border), (1, west_border)):
            for g in range(n_gy):
                @pl.when(border | (gy == g))
                def _(side=side, g=g):
                    col_copy(t, side, g).start()

        @pl.when(has_north)
        def _():
            row_copy(t, 0).start()

        @pl.when(has_south)
        def _():
            row_copy(t, 1).start()

    def wait_cols(border, sem):
        whole = from_east[0]
        part = whole.at[pl.ds(0, rows)]

        @pl.when(border)
        def _():
            pltpu.make_async_copy(whole, whole, sem).wait()

        @pl.when(jnp.logical_not(border))
        def _():
            pltpu.make_async_copy(part, part, sem).wait()

    def receive(t):
        @pl.when(has_north)
        def _():
            row_copy(t, 1).wait_recv()

        @pl.when(has_south)
        def _():
            row_copy(t, 0).wait_recv()

        for border, recv, buffer, table, col in (
            (east_border, east_recv, from_east, east_table, east_col),
            (west_border, west_recv, from_west, west_table, west_col),
        ):
            wait_cols(border, recv.at[t])

            @pl.when(border)
            def _(buffer=buffer, table=table, col=col):
                for y in range(rows):
                    col[y] = buffer[t][edge_rows[table, first_row + y]]

            @pl.when(jnp.logical_not(border))
            def _(buffer=buffer, col=col):
                col[...] = buffer[t][pl.ds(first_row, rows)]

    col_id = lax.broadcasted_iota(jnp.int32, (rows, cols, levels), 1)
    lane_id = lax.broadcasted_iota(jnp.int32, (rows * cols, levels), 1)

    def local_part(z):
        flat_z = flat(z)
        up = jnp.where(lane_id < levels - 1, pltpu.roll(flat_z, levels - 1, 1), 0.0)
        down = jnp.where(lane_id > 0, pltpu.roll(flat_z, 1, 1), 0.0)
        column = (up + down).reshape(rows, cols, levels)
        v = vert[...].reshape(1, 1, levels)
        return diag[...] * z + v * (2.0 * z - column)

    def image_of(t, z, base):
        east = jnp.where(col_id == cols - 1, east_col[...], pltpu.roll(z, cols - 1, 1))
        west = jnp.where(col_id == 0, west_col[...], pltpu.roll(z, 1, 1))
        north = jnp.concatenate([z[1:], from_north[t][None]], 0)
        south = jnp.concatenate([from_south[t][None], z[:-1]], 0)
        return base + horiz[...] * (4.0 * z - (east + west + north + south))

    def product(a, b):
        both = (a * b).reshape(rows * cols // 8, 8, levels)
        return jnp.sum(jnp.sum(both, axis=0), axis=0, keepdims=True)

    loads[0].wait()
    loads[1].wait()
    terms = {}
    spaces = [r0]
    for t in range(ITERS):
        z = precondition(spaces[-1][...])
        fields[t] = z
        send_cols[t, 0] = z[:, cols - 1 : cols, :]
        send_cols[t, 1] = z[:, 0:1, :]
        if t == 0:
            pl.semaphore_wait(barrier, n_all - 1)
        send(t)
        if t == 0:
            for load in loads[2:]:
                load.wait()
        newest = len(spaces) - 1
        for i in range(len(spaces)):
            terms[(i, newest)] = product(spaces[i][...], spaces[newest][...])
        base = local_part(z)
        receive(t)
        images[t] = image_of(t, z, base)
        spaces.append(images.at[t])
    newest = len(spaces) - 1
    for i in range(len(spaces)):
        terms[(i, newest)] = product(spaces[i][...], spaces[newest][...])

    keys = list(terms)
    height = -(-len(keys) // 8) * 8
    row_id = lax.broadcasted_iota(jnp.int32, (height, levels), 0)
    lane = lax.broadcasted_iota(jnp.int32, (height, levels), 1)
    stacked = jnp.zeros((height, levels), jnp.float32)
    for k, key in enumerate(keys):
        stacked = jnp.where(row_id == k, terms[key], stacked)
    summed = jnp.sum(stacked, axis=1, keepdims=True)
    sums[me] = jnp.sum(jnp.where(lane == row_id, summed, 0.0), axis=0, keepdims=True)

    def tell(x, y):
        pltpu.make_async_remote_copy(
            src_ref=sums.at[me],
            dst_ref=sums.at[me],
            send_sem=sum_send,
            recv_sem=sum_recv,
            device_id=(x, y),
            device_id_type=MESH,
        ).start()

    for_others(tell)
    others = sums.at[pl.ds(0, n_all - 1)]
    pltpu.make_async_copy(others, others, sum_recv).wait()
    totals = jnp.sum(sums[...], axis=0)
    value = {key: totals[:, k : k + 1] for k, key in enumerate(keys)}

    rho, g0, g1, g2 = value[(0, 0)], value[(0, 1)], value[(0, 2)], value[(0, 3)]
    a00, a01, a02 = value[(1, 1)], value[(1, 2)], value[(1, 3)]
    a11, a12, a22 = value[(2, 2)], value[(2, 3)], value[(3, 3)]
    l10, l20, y0 = a01 / a00, a02 / a00, g0 / a00
    d1, e12, f1 = a11 - l10 * a01, a12 - l10 * a02, g1 - l10 * g0
    l21, y1 = e12 / d1, f1 / d1
    d2, f2 = a22 - l20 * a02 - l21 * e12, g2 - l20 * g0 - l21 * f1
    y2 = f2 / d2
    norm0 = rho - y0 * g0
    norm1 = norm0 - y1 * f1
    norm2 = norm1 - y2 * f2
    y1 = y1 - l21 * y2
    y0 = y0 - l10 * y1 - l20 * y2
    y0, y1, y2 = [c.reshape(1, 1, 1) for c in (y0, y1, y2)]
    out_x[...] = y0 * fields[0] + y1 * fields[1] + y2 * fields[2]
    out_r[...] = r0[...] - y0 * images[0] - y1 * images[1] - y2 * images[2]
    norm_lane = lax.broadcasted_iota(jnp.int32, (1, levels), 1)
    norms = jnp.where(norm_lane == 0, norm0, jnp.where(norm_lane == 1, norm1, norm2))
    out_norms[...] = norms / total_cells

    for t in range(ITERS):
        wait_cols(east_border, col_send.at[t, 0])
        wait_cols(west_border, col_send.at[t, 1])

        @pl.when(has_north)
        def _(t=t):
            row_copy(t, 0).wait_send()

        @pl.when(has_south)
        def _(t=t):
            row_copy(t, 1).wait_send()

    pltpu.make_async_copy(others, others, sum_send).wait()


def on_device(n_gx, n_gy, right_side, diagonal, horizontal, vertical, precond, edge_rows):
    rows, cols, levels = right_side.shape
    f32 = jnp.float32
    block = (rows, cols, levels)
    sems = pltpu.SemaphoreType.DMA
    x, r, norms = pl.pallas_call(
        functools.partial(kernel, n_gx, n_gy),
        out_shape=(
            jax.ShapeDtypeStruct(block, f32),
            jax.ShapeDtypeStruct(block, f32),
            jax.ShapeDtypeStruct((1, levels), f32),
        ),
        in_specs=[SMEM, ANY, ANY, ANY, ANY, ANY],
        out_specs=(VMEM, VMEM, VMEM),
        scratch_shapes=[
            pltpu.VMEM(block, f32),
            pltpu.VMEM(block, f32),
            pltpu.VMEM(block, f32),
            pltpu.VMEM((1, levels), f32),
            pltpu.VMEM((levels, levels), f32),
            pltpu.VMEM((ITERS,) + block, f32),
            pltpu.VMEM((ITERS,) + block, f32),
            pltpu.VMEM((ITERS, 2, rows, 1, levels), f32),
            [pltpu.VMEM((n_gy * rows, 1, levels), f32)] * ITERS,
            [pltpu.VMEM((n_gy * rows, 1, levels), f32)] * ITERS,
            pltpu.VMEM((ITERS, cols, levels), f32),
            pltpu.VMEM((ITERS, cols, levels), f32),
            pltpu.VMEM((rows, 1, levels), f32),
            pltpu.VMEM((rows, 1, levels), f32),
            pltpu.VMEM((n_gx * n_gy, 1, levels), f32),
            sems((5,)),
            sems((ITERS, 2)),
            sems((ITERS,)),
            sems((ITERS,)),
            sems((ITERS, 2)),
            sems((ITERS,)),
            sems((ITERS,)),
            sems(()),
            sems(()),
        ],
        compiler_params=pltpu.CompilerParams(collective_id=0, has_side_effects=True),
    )(edge_rows, right_side, diagonal, horizontal, vertical.reshape(1, levels), precond)
    return x, r, norms[0, :ITERS]


def solution(mesh):
    n_gx, n_gy = mesh.shape["gx"], mesh.shape["gy"]
    field = P("gy", "gx", None)
    return jax.shard_map(
        functools.partial(on_device, n_gx, n_gy),
        mesh=mesh,
        in_specs=(field, field, field, P(), P(), P()),
        out_specs=(field, field, P()),
        check_vma=False,
    )
```

time: 244 us -> 32.9 us (0.13)
  blocking collectives: 175 us -> 0 us
  Pallas kernels: 0 us -> 28.6 us
  starting transfers between devices: 28.6 us -> 0 us
  other arithmetic: 12.7 us -> 0 us
  local copies, waits for them, and re-layouts: 15.2 us -> 3.44 us
  between operations: 9.45 us -> 0.65 us
    psum x4 -> x0, blocking collectives: 158 us -> none  [the longest x3 116 us: on_device(): totals = lax.psum(jnp.stack(terms), ('gx', 'gy')) / total_cells]
    ppermute x12 -> x0, starting transfers between devices: 28.6 us -> none  [the longest x6 16.8 us: padded(): before = lax.ppermute(last, axis, up)]
    pallas_call x0 -> x1, Pallas kernels: none -> 28.6 us  [on_device(): pl.pallas_call(functools.partial(kernel, n_gx, n_gy), out_shape=(jax.Shap...]
    all_gather x3 -> x0, blocking collectives: 17 us -> none  [on_device(): whole = lax.all_gather(edges, 'gy', axis=1, tiled=True)]
    another operation x2 -> x0, local copies, waits for them, and re-layouts: 7.69 us -> none  [on_device(): totals = lax.psum(jnp.stack(terms), ('gx', 'gy')) / total_cells]
    reduce_sum x5 -> x0, other arithmetic: 5.7 us -> none  [the longest x4 4.94 us: local_product(): return jnp.sum(left * right)]
    gather x6 -> x0, local copies, waits for them, and re-layouts: 3.37 us -> none  [the longest x3 1.69 us: on_device(): west_fix = jnp.take(whole[0], west_local, axis=0)]
    another operation x5 -> x0, other arithmetic: 3.15 us -> none  [the longest x1 1.78 us: on_device(): return (solution_field, residual, jnp.stack(norms))]
  transfers between devices with their start and end apart: 12 -> 0, of which waited for: 1 -> 0; matrix products, arithmetic and copies ran while one was open for 2% -> 0% of each run, Pallas kernels for 0% -> 0%
where the time goes in v1:
time: 32.9 us; the launch traced here: 32.7 us
  Pallas kernels  28.6 us (87%)
  local copies, waits for them, and re-layouts  3.44 us (10%)
  between operations  0.65 us (2%)
    pallas_call x1, Pallas kernels, on_device(): pl.pallas_call(functools.partial(kernel, n_gx, n_gy), out_shape=(jax.Shap...  28.6 us
    unnamed x6, local copies, waits for them, and re-layouts  2.93 us

profile of v1, /device:TPU:0, one launch (start us, length us, event | category | flops | bytes accessed | tf_op | source)
XLA Modules:
  0.0 32.7 jit_solution(10574463906467073226)
XLA Ops:
  0.6 28.6 %shard_map.85 = (f32[16,16,128]{2,1,0:T(8,128)}, f32[16,16,128]{2,1,0:T(8,128)}, f32[1,128]{1,0:T(1,128)}) custom-call(s32[2,64]{1,0:T(2,128)} %edge_rows.1, f32[16,16,128]{2,1,0:T(8,128)} %right_side.1, f32[16,16,128]{2,1,0:T(8,128)} %diagonal.1, f32[16,16,128]{2,1,0:T(8,128)} %horizontal.1, f32[1,128]{1,0:T(1,128)} %bitcast.3, f32[2,128,128]{2,1,0:T(8,128)} %precond.1), custom_call_target="tpu_custom_call" | custom-call | tf_op jit(solution)/shard_map/pallas_call | solution.py:315
  29.3 0.0 copy-start.1
  29.3 0.7 %copy-done.1 = f32[1,128]{1,0:T(1,128)S(1)} copy-done((f32[1,128]{1,0:T(1,128)S(1)}, f32[1,128]{1,0:T(1,128)}, u32[]{:S(2)}) %copy-start.1) | copy-done | bytes 536
  29.9 0.5 %slice_bitcast_fusion = f32[3]{0:T(128)} fusion(f32[1,128]{1,0:T(1,128)S(1)} %copy-done.1), kind=kLoop, calls=%fused_computation | loop fusion | bytes 24 | tf_op jit(solution)/shard_map/squeeze | solution.py:352
  30.4 0.0 copy-start
  30.5 1.6 %copy.11 = f32[16,16,128]{2,1,0:T(8,128)} copy(f32[16,16,128]{2,1,0:T(8,128)} %get-tuple-element.12) | data formatting | bytes 262144
  32.1 0.0 copy-done
  32.1 0.7 %copy.12 = f32[16,16,128]{2,1,0:T(8,128)} copy(f32[16,16,128]{2,1,0:T(8,128)S(1)} %copy-done) | data formatting | bytes 262144
Async XLA Ops:
  29.3 0.7 %copy-start.1 = (f32[1,128]{1,0:T(1,128)S(1)}, f32[1,128]{1,0:T(1,128)}, u32[]{:S(2)}) copy-start(f32[1,128]{1,0:T(1,128)} %get-tuple-element.8) | copy-start | bytes 1540
  30.4 1.6 %copy-start = (f32[16,16,128]{2,1,0:T(8,128)S(1)}, f32[16,16,128]{2,1,0:T(8,128)}, u32[]{:S(2)}) copy-start(f32[16,16,128]{2,1,0:T(8,128)} %get-tuple-element.13) | copy-start | bytes 393220

commit v2 on v1

--- a/solution.py
+++ b/solution.py
@@ -8,6 +8,7 @@
 from jax.sharding import PartitionSpec as P
 
 ITERS = 3
+KEYS = [(i, j) for j in range(ITERS + 1) for i in range(j + 1)]
 MESH = pl.DeviceIdType.MESH
 ANY = pl.BlockSpec(memory_space=pl.ANY)
 VMEM = pl.BlockSpec(memory_space=pltpu.VMEM)
@@ -23,16 +24,14 @@
     horizontal,
     vertical,
     precond,
-    out_x,
-    out_r,
-    out_norms,
+    fields,
+    images,
+    out_totals,
     r0,
     diag,
     horiz,
     vert,
     matrix,
-    fields,
-    images,
     send_cols,
     from_east,
     from_west,
@@ -56,7 +55,6 @@
     n_all = n_gx * n_gy
     half = n_gx // 2
     me = gx * n_gy + gy
-    total_cells = float(rows * cols * levels * n_all)
 
     def for_others(visit):
         for j in range(1, n_gy):
@@ -246,7 +244,7 @@
     for i in range(len(spaces)):
         terms[(i, newest)] = product(spaces[i][...], spaces[newest][...])
 
-    keys = list(terms)
+    keys = KEYS
     height = -(-len(keys) // 8) * 8
     row_id = lax.broadcasted_iota(jnp.int32, (height, levels), 0)
     lane = lax.broadcasted_iota(jnp.int32, (height, levels), 1)
@@ -269,8 +267,27 @@
     for_others(tell)
     others = sums.at[pl.ds(0, n_all - 1)]
     pltpu.make_async_copy(others, others, sum_recv).wait()
-    totals = jnp.sum(sums[...], axis=0)
-    value = {key: totals[:, k : k + 1] for k, key in enumerate(keys)}
+    out_totals[...] = jnp.sum(sums[...], axis=0)
+
+    for t in range(ITERS):
+        wait_cols(east_border, col_send.at[t, 0])
+        wait_cols(west_border, col_send.at[t, 1])
+
+        @pl.when(has_north)
+        def _(t=t):
+            row_copy(t, 0).wait_send()
+
+        @pl.when(has_south)
+        def _(t=t):
+            row_copy(t, 1).wait_send()
+
+    pltpu.make_async_copy(others, others, sum_send).wait()
+
+
+def finish(total_cells, all_totals, r0, fields, images, out_x, out_r, out_norms, x, r, sem):
+    levels = r0.shape[-1]
+    totals = all_totals[...]
+    value = {key: totals[:, k : k + 1] for k, key in enumerate(KEYS)}
 
     rho, g0, g1, g2 = value[(0, 0)], value[(0, 1)], value[(0, 2)], value[(0, 3)]
     a00, a01, a02 = value[(1, 1)], value[(1, 2)], value[(1, 3)]
@@ -286,25 +303,25 @@
     y1 = y1 - l21 * y2
     y0 = y0 - l10 * y1 - l20 * y2
     y0, y1, y2 = [c.reshape(1, 1, 1) for c in (y0, y1, y2)]
-    out_x[...] = y0 * fields[0] + y1 * fields[1] + y2 * fields[2]
-    out_r[...] = r0[...] - y0 * images[0] - y1 * images[1] - y2 * images[2]
     norm_lane = lax.broadcasted_iota(jnp.int32, (1, levels), 1)
     norms = jnp.where(norm_lane == 0, norm0, jnp.where(norm_lane == 1, norm1, norm2))
-    out_norms[...] = norms / total_cells
-
-    for t in range(ITERS):
-        wait_cols(east_border, col_send.at[t, 0])
-        wait_cols(west_border, col_send.at[t, 1])
-
-        @pl.when(has_north)
-        def _(t=t):
-            row_copy(t, 0).wait_send()
-
-        @pl.when(has_south)
-        def _(t=t):
-            row_copy(t, 1).wait_send()
-
-    pltpu.make_async_copy(others, others, sum_send).wait()
+    out_norms[...] = norms[:, :ITERS] / total_cells
+    rows = r0.shape[0]
+    pieces = 2 if rows % 2 == 0 else 1
+    size = rows // pieces
+    copies = []
+    for p in range(pieces):
+        span = pl.ds(p * size, size)
+        x[span] = y0 * fields[0, span] + y1 * fields[1, span] + y2 * fields[2, span]
+        r[span] = (
+            r0[span] - y0 * images[0, span] - y1 * images[1, span] - y2 * images[2, span]
+        )
+        for k, (src, dst) in enumerate(((x, out_x), (r, out_r))):
+            copy = pltpu.make_async_copy(src.at[span], dst.at[span], sem.at[p, k])
+            copy.start()
+            copies.append(copy)
+    for copy in copies:
+        copy.wait()
 
 
 def on_device(n_gx, n_gy, right_side, diagonal, horizontal, vertical, precond, edge_rows):
@@ -312,23 +329,17 @@
     f32 = jnp.float32
     block = (rows, cols, levels)
     sems = pltpu.SemaphoreType.DMA
-    x, r, norms = pl.pallas_call(
+    basis = pltpu.VMEM((ITERS,) + block, f32)
+    fields, images, totals, start = pl.pallas_call(
         functools.partial(kernel, n_gx, n_gy),
-        out_shape=(
-            jax.ShapeDtypeStruct(block, f32),
-            jax.ShapeDtypeStruct(block, f32),
-            jax.ShapeDtypeStruct((1, levels), f32),
-        ),
+        out_shape=(basis, basis, pltpu.VMEM((1, levels), f32), pltpu.VMEM(block, f32)),
         in_specs=[SMEM, ANY, ANY, ANY, ANY, ANY],
-        out_specs=(VMEM, VMEM, VMEM),
+        out_specs=(VMEM, VMEM, VMEM, VMEM),
         scratch_shapes=[
-            pltpu.VMEM(block, f32),
             pltpu.VMEM(block, f32),
             pltpu.VMEM(block, f32),
             pltpu.VMEM((1, levels), f32),
             pltpu.VMEM((levels, levels), f32),
-            pltpu.VMEM((ITERS,) + block, f32),
-            pltpu.VMEM((ITERS,) + block, f32),
             pltpu.VMEM((ITERS, 2, rows, 1, levels), f32),
             [pltpu.VMEM((n_gy * rows, 1, levels), f32)] * ITERS,
             [pltpu.VMEM((n_gy * rows, 1, levels), f32)] * ITERS,
@@ -349,7 +360,22 @@
         ],
         compiler_params=pltpu.CompilerParams(collective_id=0, has_side_effects=True),
     )(edge_rows, right_side, diagonal, horizontal, vertical.reshape(1, levels), precond)
-    return x, r, norms[0, :ITERS]
+    in_vmem = functools.partial(
+        pltpu.with_memory_space_constraint, memory_space=pltpu.VMEM
+    )
+    total_cells = float(rows * cols * levels * n_gx * n_gy)
+    x, r, norms = pl.pallas_call(
+        functools.partial(finish, total_cells),
+        out_shape=(
+            jax.ShapeDtypeStruct(block, f32),
+            jax.ShapeDtypeStruct(block, f32),
+            jax.ShapeDtypeStruct((1, ITERS), f32),
+        ),
+        in_specs=[VMEM, VMEM, VMEM, VMEM],
+        out_specs=(ANY, ANY, VMEM),
+        scratch_shapes=[pltpu.VMEM(block, f32), pltpu.VMEM(block, f32), sems((2, 2))],
+    )(in_vmem(totals), in_vmem(start), in_vmem(fields), in_vmem(images))
+    return x, r, norms.reshape(ITERS)
 
 
 def solution(mesh):

time: 32.9 us -> 29.9 us (0.909)
  local copies, waits for them, and re-layouts: 3.44 us -> 0 us
  Pallas kernels: 28.6 us -> 29.1 us
    unnamed x6 -> x0, local copies, waits for them, and re-layouts: 2.93 us -> none
    squeeze x1 -> x0, local copies, waits for them, and re-layouts: 0.51 us -> none  [on_device(): return (x, r, norms[0, :ITERS])]
    pallas_call x1 -> x2, Pallas kernels: 28.6 us -> 29.1 us  [the longest x1 27.1 us: on_device(): pl.pallas_call(functools.partial(kernel, n_gx, n_gy), out_shape=(basis, b...]
where the time goes in v2:
time: 29.9 us; the launch traced here: 29.7 us
  Pallas kernels  29.1 us (97%)
  between operations  0.64 us (2%)
    pallas_call x1, Pallas kernels, on_device(): pl.pallas_call(functools.partial(kernel, n_gx, n_gy), out_shape=(basis, b...  27.1 us
    pallas_call x1, Pallas kernels, on_device(): pl.pallas_call(functools.partial(finish, total_cells), out_shape=(jax.Sha...  1.96 us

profile of v2, /device:TPU:0, one launch (start us, length us, event | category | flops | bytes accessed | tf_op | source)
XLA Modules:
  0.0 29.7 jit_solution(10864086836239343132)
XLA Ops:
  0.6 27.1 %shard_map.85 = (f32[3,16,16,128]{3,2,1,0:T(8,128)S(1)}, f32[3,16,16,128]{3,2,1,0:T(8,128)S(1)}, f32[1,128]{1,0:T(1,128)S(1)}, f32[16,16,128]{2,1,0:T(8,128)S(1)}) custom-call(s32[2,64]{1,0:T(2,128)} %edge_rows.1, f32[16,16,128]{2,1,0:T(8,128)} %right_side.1, f32[16,16,128]{2,1,0:T(8,128)} %diagonal.1, f32[16,16,128]{2,1,0:T(8,128)} %horizontal.1, ...), custom_call_target="tpu_custom_call" | custom-call | tf_op jit(solution)/shard_map/pallas_call | solution.py:333
  27.8 2.0 %shard_map.86 = (f32[16,16,128]{2,1,0:T(8,128)}, f32[16,16,128]{2,1,0:T(8,128)}, f32[1,3]{1,0:T(1,128)}) custom-call(f32[1,128]{1,0:T(1,128)S(1)} %get-tuple-element.10.all_totals, f32[16,16,128]{2,1,0:T(8,128)S(1)} %get-tuple-element.11.r0, f32[3,16,16,128]{3,2,1,0:T(8,128)S(1)} %get-tuple-element.12.fields, f32[3,16,16,128]{3,2,1,0:T(8,128)S(1)} %get-tuple-element.13.images), custom_call_target="tpu_custom_call" | custom-call | tf_op jit(solution)/shard_map/pallas_call | solution.py:367

commit v3 on v2

--- a/solution.py
+++ b/solution.py
@@ -18,6 +18,7 @@
 def kernel(
     n_gx,
     n_gy,
+    out_rows,
     edge_rows,
     right_side,
     diagonal,
@@ -37,8 +38,7 @@
     from_west,
     from_north,
     from_south,
-    east_col,
-    west_col,
+    outside,
     sums,
     load_sem,
     col_send,
@@ -50,7 +50,9 @@
     sum_send,
     sum_recv,
 ):
-    rows, cols, levels = r0.shape
+    rows, levels = out_rows, r0.shape[-1]
+    cells = r0.shape[0]
+    cols = cells // rows
     gx, gy = lax.axis_index("gx"), lax.axis_index("gy")
     n_all = n_gx * n_gy
     half = n_gx // 2
@@ -105,24 +107,21 @@
     def _():
         from_south[...] = jnp.zeros_like(from_south)
 
-    def flat(v):
-        return v.reshape(rows * cols, levels)
-
     def precondition(v):
         return lax.dot_general(
-            flat(v),
+            v,
             matrix[...],
             (((1,), (1,)), ((), ())),
             precision=lax.Precision.HIGHEST,
             preferred_element_type=jnp.float32,
-        ).reshape(rows, cols, levels)
+        )
 
     def col_copy(t, side, g):
         buffer, recv, x = (
             (from_west, west_recv, east_x) if side == 0 else (from_east, east_recv, west_x)
         )
         return pltpu.make_async_remote_copy(
-            src_ref=send_cols.at[t, side],
+            src_ref=send_cols.at[t, pl.ds(side * rows, rows)],
             dst_ref=buffer[t].at[pl.ds(first_row, rows)],
             send_sem=col_send.at[t, side],
             recv_sem=recv.at[t],
@@ -132,12 +131,12 @@
 
     def row_copy(t, side):
         buffer, recv, y, row = (
-            (from_south, south_recv, gy + 1, rows - 1)
+            (from_south, south_recv, gy + 1, cells - cols)
             if side == 0
             else (from_north, north_recv, gy - 1, 0)
         )
         return pltpu.make_async_remote_copy(
-            src_ref=fields.at[t, row],
+            src_ref=fields.at[t, pl.ds(row, cols)],
             dst_ref=buffer.at[t],
             send_sem=row_send.at[t, side],
             recv_sem=recv.at[t],
@@ -145,13 +144,17 @@
             device_id_type=MESH,
         )
 
-    def send(t):
+    def send_cols_on(t, edges):
+        send_cols[t] = precondition(edges)
+        if t == 0:
+            pl.semaphore_wait(barrier, n_all - 1)
         for side, border in ((0, east_border), (1, west_border)):
             for g in range(n_gy):
                 @pl.when(border | (gy == g))
                 def _(side=side, g=g):
                     col_copy(t, side, g).start()
 
+    def send_rows(t):
         @pl.when(has_north)
         def _():
             row_copy(t, 0).start()
@@ -172,7 +175,7 @@
         def _():
             pltpu.make_async_copy(part, part, sem).wait()
 
-    def receive(t):
+    def receive_rows(t):
         @pl.when(has_north)
         def _():
             row_copy(t, 1).wait_recv()
@@ -181,65 +184,81 @@
         def _():
             row_copy(t, 0).wait_recv()
 
-        for border, recv, buffer, table, col in (
-            (east_border, east_recv, from_east, east_table, east_col),
-            (west_border, west_recv, from_west, west_table, west_col),
+    def receive_cols(t):
+        for border, recv, buffer, table, part in (
+            (east_border, east_recv, from_east, east_table, 0),
+            (west_border, west_recv, from_west, west_table, rows),
         ):
             wait_cols(border, recv.at[t])
 
             @pl.when(border)
-            def _(buffer=buffer, table=table, col=col):
+            def _(buffer=buffer, table=table, part=part):
                 for y in range(rows):
-                    col[y] = buffer[t][edge_rows[table, first_row + y]]
+                    row = edge_rows[table, first_row + y]
+                    outside[pl.ds(part + y, 1), :] = buffer[t][pl.ds(row, 1), :]
 
             @pl.when(jnp.logical_not(border))
-            def _(buffer=buffer, col=col):
-                col[...] = buffer[t][pl.ds(first_row, rows)]
-
-    col_id = lax.broadcasted_iota(jnp.int32, (rows, cols, levels), 1)
-    lane_id = lax.broadcasted_iota(jnp.int32, (rows * cols, levels), 1)
-
-    def local_part(z):
-        flat_z = flat(z)
-        up = jnp.where(lane_id < levels - 1, pltpu.roll(flat_z, levels - 1, 1), 0.0)
-        down = jnp.where(lane_id > 0, pltpu.roll(flat_z, 1, 1), 0.0)
-        column = (up + down).reshape(rows, cols, levels)
-        v = vert[...].reshape(1, 1, levels)
-        return diag[...] * z + v * (2.0 * z - column)
-
-    def image_of(t, z, base):
-        east = jnp.where(col_id == cols - 1, east_col[...], pltpu.roll(z, cols - 1, 1))
-        west = jnp.where(col_id == 0, west_col[...], pltpu.roll(z, 1, 1))
-        north = jnp.concatenate([z[1:], from_north[t][None]], 0)
-        south = jnp.concatenate([from_south[t][None], z[:-1]], 0)
-        return base + horiz[...] * (4.0 * z - (east + west + north + south))
+            def _(buffer=buffer, part=part):
+                outside[pl.ds(part, rows), :] = buffer[t][pl.ds(first_row, rows), :]
+
+    col_id = lax.rem(lax.broadcasted_iota(jnp.int32, (cells, levels), 0), cols)
+    lane_id = lax.broadcasted_iota(jnp.int32, (cells, levels), 1)
+    east_edge = pl.ds(cols - 1, rows, stride=cols)
+    west_edge = pl.ds(0, rows, stride=cols)
+    south_edge = pl.ds(0, cols)
+    north_edge = pl.ds(cells - cols, cols)
+
+    def edge_columns(ref):
+        return jnp.concatenate([ref[east_edge, :], ref[west_edge, :]], 0)
+
+    def inner_image(z):
+        up = jnp.where(lane_id < levels - 1, pltpu.roll(z, levels - 1, 1), 0.0)
+        down = jnp.where(lane_id > 0, pltpu.roll(z, 1, 1), 0.0)
+        east = jnp.where(col_id < cols - 1, pltpu.roll(z, cells - 1, 0), 0.0)
+        west = jnp.where(col_id > 0, pltpu.roll(z, 1, 0), 0.0)
+        none = jnp.zeros((cols, levels), jnp.float32)
+        north = jnp.concatenate([z[cols:], none], 0)
+        south = jnp.concatenate([none, z[:-cols]], 0)
+        beside = east + west + north + south
+        return (
+            diag[...] * z
+            + horiz[...] * (4.0 * z - beside)
+            + vert[...] * (2.0 * z - (up + down))
+        )
 
     def product(a, b):
-        both = (a * b).reshape(rows * cols // 8, 8, levels)
+        both = (a * b).reshape(cells // 8, 8, levels)
         return jnp.sum(jnp.sum(both, axis=0), axis=0, keepdims=True)
 
     loads[0].wait()
     loads[1].wait()
     terms = {}
     spaces = [r0]
+    send_cols_on(0, edge_columns(r0))
     for t in range(ITERS):
+        image = images.at[t]
         z = precondition(spaces[-1][...])
         fields[t] = z
-        send_cols[t, 0] = z[:, cols - 1 : cols, :]
-        send_cols[t, 1] = z[:, 0:1, :]
-        if t == 0:
-            pl.semaphore_wait(barrier, n_all - 1)
-        send(t)
+        send_rows(t)
         if t == 0:
             for load in loads[2:]:
                 load.wait()
+            edge_horiz = edge_columns(horiz)
         newest = len(spaces) - 1
         for i in range(len(spaces)):
             terms[(i, newest)] = product(spaces[i][...], spaces[newest][...])
-        base = local_part(z)
-        receive(t)
-        images[t] = image_of(t, z, base)
-        spaces.append(images.at[t])
+        image[...] = inner_image(z)
+        receive_rows(t)
+        image[south_edge, :] = image[south_edge, :] - horiz[south_edge, :] * from_south[t]
+        image[north_edge, :] = image[north_edge, :] - horiz[north_edge, :] * from_north[t]
+        inside = edge_columns(image)
+        receive_cols(t)
+        edges = inside - edge_horiz * outside[...]
+        if t < ITERS - 1:
+            send_cols_on(t + 1, edges)
+        image[east_edge, :] = edges[:rows]
+        image[west_edge, :] = edges[rows:]
+        spaces.append(image)
     newest = len(spaces) - 1
     for i in range(len(spaces)):
         terms[(i, newest)] = product(spaces[i][...], spaces[newest][...])
@@ -302,12 +321,11 @@
     norm2 = norm1 - y2 * f2
     y1 = y1 - l21 * y2
     y0 = y0 - l10 * y1 - l20 * y2
-    y0, y1, y2 = [c.reshape(1, 1, 1) for c in (y0, y1, y2)]
     norm_lane = lax.broadcasted_iota(jnp.int32, (1, levels), 1)
     norms = jnp.where(norm_lane == 0, norm0, jnp.where(norm_lane == 1, norm1, norm2))
     out_norms[...] = norms[:, :ITERS] / total_cells
     rows = r0.shape[0]
-    pieces = 2 if rows % 2 == 0 else 1
+    pieces = 2 if rows % 16 == 0 else 1
     size = rows // pieces
     copies = []
     for p in range(pieces):
@@ -327,11 +345,11 @@
 def on_device(n_gx, n_gy, right_side, diagonal, horizontal, vertical, precond, edge_rows):
     rows, cols, levels = right_side.shape
     f32 = jnp.float32
-    block = (rows, cols, levels)
+    block = (rows * cols, levels)
     sems = pltpu.SemaphoreType.DMA
     basis = pltpu.VMEM((ITERS,) + block, f32)
     fields, images, totals, start = pl.pallas_call(
-        functools.partial(kernel, n_gx, n_gy),
+        functools.partial(kernel, n_gx, n_gy, rows),
         out_shape=(basis, basis, pltpu.VMEM((1, levels), f32), pltpu.VMEM(block, f32)),
         in_specs=[SMEM, ANY, ANY, ANY, ANY, ANY],
         out_specs=(VMEM, VMEM, VMEM, VMEM),
@@ -340,13 +358,12 @@
             pltpu.VMEM(block, f32),
             pltpu.VMEM((1, levels), f32),
             pltpu.VMEM((levels, levels), f32),
-            pltpu.VMEM((ITERS, 2, rows, 1, levels), f32),
-            [pltpu.VMEM((n_gy * rows, 1, levels), f32)] * ITERS,
-            [pltpu.VMEM((n_gy * rows, 1, levels), f32)] * ITERS,
+            pltpu.VMEM((ITERS, 2 * rows, levels), f32),
+            [pltpu.VMEM((n_gy * rows, levels), f32)] * ITERS,
+            [pltpu.VMEM((n_gy * rows, levels), f32)] * ITERS,
             pltpu.VMEM((ITERS, cols, levels), f32),
             pltpu.VMEM((ITERS, cols, levels), f32),
-            pltpu.VMEM((rows, 1, levels), f32),
-            pltpu.VMEM((rows, 1, levels), f32),
+            pltpu.VMEM((2 * rows, levels), f32),
             pltpu.VMEM((n_gx * n_gy, 1, levels), f32),
             sems((5,)),
             sems((ITERS, 2)),
@@ -359,7 +376,14 @@
             sems(()),
         ],
         compiler_params=pltpu.CompilerParams(collective_id=0, has_side_effects=True),
-    )(edge_rows, right_side, diagonal, horizontal, vertical.reshape(1, levels), precond)
+    )(
+        edge_rows,
+        right_side.reshape(block),
+        diagonal.reshape(block),
+        horizontal.reshape(block),
+        vertical.reshape(1, levels),
+        precond,
+    )
     in_vmem = functools.partial(
         pltpu.with_memory_space_constraint, memory_space=pltpu.VMEM
     )
@@ -375,7 +399,8 @@
         out_specs=(ANY, ANY, VMEM),
         scratch_shapes=[pltpu.VMEM(block, f32), pltpu.VMEM(block, f32), sems((2, 2))],
     )(in_vmem(totals), in_vmem(start), in_vmem(fields), in_vmem(images))
-    return x, r, norms.reshape(ITERS)
+    shape = right_side.shape
+    return x.reshape(shape), r.reshape(shape), norms.reshape(ITERS)
 
 
 def solution(mesh):

time: 29.9 us -> 29.7 us (level)
  no operation moved by 1% of the time
where the time goes in v3:
time: 29.7 us; the launch traced here: 29.6 us
  Pallas kernels  28.9 us (97%)
  between operations  0.64 us (2%)
    pallas_call x1, Pallas kernels, on_device(): pl.pallas_call(functools.partial(kernel, n_gx, n_gy, rows), out_shape=(ba...  27 us
    pallas_call x1, Pallas kernels, on_device(): pl.pallas_call(functools.partial(finish, total_cells), out_shape=(jax.Sha...  1.96 us

profile of v3, /device:TPU:0, one launch (start us, length us, event | category | flops | bytes accessed | tf_op | source)
XLA Modules:
  0.0 29.6 jit_solution(2974938423384103568)
XLA Ops:
  0.6 27.0 %shard_map.85 = (f32[3,256,128]{2,1,0:T(8,128)S(1)}, f32[3,256,128]{2,1,0:T(8,128)S(1)}, f32[1,128]{1,0:T(1,128)S(1)}, f32[256,128]{1,0:T(8,128)S(1)}) custom-call(s32[2,64]{1,0:T(2,128)} %edge_rows.1, f32[256,128]{1,0:T(8,128)} %bitcast.7, f32[256,128]{1,0:T(8,128)} %bitcast.8, f32[256,128]{1,0:T(8,128)} %bitcast.9, f32[1,128]{1,0:T(1,128)} %bitcast.10, ...), custom_call_target="tpu_custom_call" | custom-call | tf_op jit(solution)/shard_map/pallas_call | solution.py:351
  27.6 2.0 %shard_map.86 = (f32[256,128]{1,0:T(8,128)}, f32[256,128]{1,0:T(8,128)}, f32[1,3]{1,0:T(1,128)}) custom-call(f32[1,128]{1,0:T(1,128)S(1)} %get-tuple-element.10.all_totals, f32[256,128]{1,0:T(8,128)S(1)} %get-tuple-element.11.r0, f32[3,256,128]{2,1,0:T(8,128)S(1)} %get-tuple-element.12.fields, f32[3,256,128]{2,1,0:T(8,128)S(1)} %get-tuple-element.13.images), custom_call_target="tpu_custom_call" | custom-call | tf_op jit(solution)/shard_map/pallas_call | solution.py:391

commit v4 on v3

--- a/solution.py
+++ b/solution.py
@@ -12,14 +12,13 @@
 MESH = pl.DeviceIdType.MESH
 ANY = pl.BlockSpec(memory_space=pl.ANY)
 VMEM = pl.BlockSpec(memory_space=pltpu.VMEM)
-SMEM = pl.BlockSpec(memory_space=pltpu.SMEM)
 
 
 def kernel(
     n_gx,
     n_gy,
     out_rows,
-    edge_rows,
+    edge_table,
     right_side,
     diagonal,
     horizontal,
@@ -40,6 +39,7 @@
     from_south,
     outside,
     sums,
+    edge_rows,
     load_sem,
     col_send,
     east_recv,
@@ -87,6 +87,7 @@
         pltpu.make_async_copy(diagonal, diag, load_sem.at[2]),
         pltpu.make_async_copy(horizontal, horiz, load_sem.at[3]),
         pltpu.make_async_copy(vertical, vert, load_sem.at[4]),
+        pltpu.make_async_copy(edge_table, edge_rows, load_sem.at[5]),
     ]
     for load in loads:
         load.start()
@@ -351,7 +352,7 @@
     fields, images, totals, start = pl.pallas_call(
         functools.partial(kernel, n_gx, n_gy, rows),
         out_shape=(basis, basis, pltpu.VMEM((1, levels), f32), pltpu.VMEM(block, f32)),
-        in_specs=[SMEM, ANY, ANY, ANY, ANY, ANY],
+        in_specs=[ANY, ANY, ANY, ANY, ANY, ANY],
         out_specs=(VMEM, VMEM, VMEM, VMEM),
         scratch_shapes=[
             pltpu.VMEM(block, f32),
@@ -365,7 +366,8 @@
             pltpu.VMEM((ITERS, cols, levels), f32),
             pltpu.VMEM((2 * rows, levels), f32),
             pltpu.VMEM((n_gx * n_gy, 1, levels), f32),
-            sems((5,)),
+            pltpu.SMEM(edge_rows.shape, jnp.int32),
+            sems((6,)),
             sems((ITERS, 2)),
             sems((ITERS,)),
             sems((ITERS,)),

time: 29.7 us -> 29 us (0.976)
  Pallas kernels: 28.9 us -> 28.2 us
    pallas_call x1, Pallas kernels: 27 us -> 26.3 us  [on_device(): pl.pallas_call(functools.partial(kernel, n_gx, n_gy, rows), out_shape=(ba...]
where the time goes in v4:
time: 29 us; the launch traced here: 28.9 us
  Pallas kernels  28.2 us (97%)
  between operations  0.64 us (2%)
    pallas_call x1, Pallas kernels, on_device(): pl.pallas_call(functools.partial(kernel, n_gx, n_gy, rows), out_shape=(ba...  26.3 us
    pallas_call x1, Pallas kernels, on_device(): pl.pallas_call(functools.partial(finish, total_cells), out_shape=(jax.Sha...  1.96 us

profile of v4, /device:TPU:0, one launch (start us, length us, event | category | flops | bytes accessed | tf_op | source)
XLA Modules:
  0.0 28.9 jit_solution(14613782972541140)
XLA Ops:
  0.6 26.3 %shard_map.85 = (f32[3,256,128]{2,1,0:T(8,128)S(1)}, f32[3,256,128]{2,1,0:T(8,128)S(1)}, f32[1,128]{1,0:T(1,128)S(1)}, f32[256,128]{1,0:T(8,128)S(1)}) custom-call(s32[2,64]{1,0:T(2,128)} %edge_table.1, f32[256,128]{1,0:T(8,128)} %bitcast.7, f32[256,128]{1,0:T(8,128)} %bitcast.8, f32[256,128]{1,0:T(8,128)} %bitcast.9, f32[1,128]{1,0:T(1,128)} %bitcast.10, ...), custom_call_target="tpu_custom_call" | custom-call | tf_op jit(solution)/shard_map/pallas_call | solution.py:352
  26.9 2.0 %shard_map.86 = (f32[256,128]{1,0:T(8,128)}, f32[256,128]{1,0:T(8,128)}, f32[1,3]{1,0:T(1,128)}) custom-call(f32[1,128]{1,0:T(1,128)S(1)} %get-tuple-element.10.all_totals, f32[256,128]{1,0:T(8,128)S(1)} %get-tuple-element.11.r0, f32[3,256,128]{2,1,0:T(8,128)S(1)} %get-tuple-element.12.fields, f32[3,256,128]{2,1,0:T(8,128)S(1)} %get-tuple-element.13.images), custom_call_target="tpu_custom_call" | custom-call | tf_op jit(solution)/shard_map/pallas_call | solution.py:393

commit v5 on v4

--- a/solution.py
+++ b/solution.py
@@ -59,19 +59,18 @@
     me = gx * n_gy + gy
 
     def for_others(visit):
-        for j in range(1, n_gy):
-            visit(gx, lax.rem(gy + j, n_gy))
-
         def step(i, carry):
             for j in range(n_gy):
                 visit(lax.rem(gx + i, n_gx), lax.rem(gy + j, n_gy))
             return carry
 
         if n_all <= 64:
-            for i in range(1, n_gx):
+            for i in sorted(range(1, n_gx), key=lambda i: min(i, n_gx - i)):
                 step(i, 0)
         else:
             lax.fori_loop(1, n_gx, step, 0)
+        for j in range(1, n_gy):
+            visit(gx, lax.rem(gy + j, n_gy))
 
     barrier = pltpu.get_barrier_semaphore()
 
@@ -150,10 +149,12 @@
         if t == 0:
             pl.semaphore_wait(barrier, n_all - 1)
         for side, border in ((0, east_border), (1, west_border)):
-            for g in range(n_gy):
-                @pl.when(border | (gy == g))
-                def _(side=side, g=g):
-                    col_copy(t, side, g).start()
+            @pl.when(border)
+            def _(side=side):
+                for j in sorted(range(1, n_gy), key=lambda j: abs(2 * j - n_gy)):
+                    col_copy(t, side, lax.rem(gy + j, n_gy)).start()
+
+            col_copy(t, side, gy).start()
 
     def send_rows(t):
         @pl.when(has_north)

time: 29 us -> 28.6 us (0.986)
  Pallas kernels: 28.2 us -> 27.8 us
    pallas_call x1, Pallas kernels: 26.3 us -> 25.9 us  [on_device(): pl.pallas_call(functools.partial(kernel, n_gx, n_gy, rows), out_shape=(ba...]
where the time goes in v5:
time: 28.6 us; the launch traced here: 28.5 us
  Pallas kernels  27.8 us (97%)
  between operations  0.64 us (2%)
    pallas_call x1, Pallas kernels, on_device(): pl.pallas_call(functools.partial(kernel, n_gx, n_gy, rows), out_shape=(ba...  25.9 us
    pallas_call x1, Pallas kernels, on_device(): pl.pallas_call(functools.partial(finish, total_cells), out_shape=(jax.Sha...  1.96 us

profile of v5, /device:TPU:0, one launch (start us, length us, event | category | flops | bytes accessed | tf_op | source)
XLA Modules:
  0.0 28.5 jit_solution(16194968669224265548)
XLA Ops:
  0.6 25.9 %shard_map.85 = (f32[3,256,128]{2,1,0:T(8,128)S(1)}, f32[3,256,128]{2,1,0:T(8,128)S(1)}, f32[1,128]{1,0:T(1,128)S(1)}, f32[256,128]{1,0:T(8,128)S(1)}) custom-call(s32[2,64]{1,0:T(2,128)} %edge_table.1, f32[256,128]{1,0:T(8,128)} %bitcast.7, f32[256,128]{1,0:T(8,128)} %bitcast.8, f32[256,128]{1,0:T(8,128)} %bitcast.9, f32[1,128]{1,0:T(1,128)} %bitcast.10, ...), custom_call_target="tpu_custom_call" | custom-call | tf_op jit(solution)/shard_map/pallas_call | solution.py:353
  26.5 2.0 %shard_map.86 = (f32[256,128]{1,0:T(8,128)}, f32[256,128]{1,0:T(8,128)}, f32[1,3]{1,0:T(1,128)}) custom-call(f32[1,128]{1,0:T(1,128)S(1)} %get-tuple-element.10.all_totals, f32[256,128]{1,0:T(8,128)S(1)} %get-tuple-element.11.r0, f32[3,256,128]{2,1,0:T(8,128)S(1)} %get-tuple-element.12.fields, f32[3,256,128]{2,1,0:T(8,128)S(1)} %get-tuple-element.13.images), custom_call_target="tpu_custom_call" | custom-call | tf_op jit(solution)/shard_map/pallas_call | solution.py:394
